TPU v7x, 32 devices: a whole 2x2x4 slice. The times are simulated.
32 devices in a mesh: dp: 4 (over z), tensor: 8 (over y, x, core).
Axes of the slice: x: 2, y: 2, z: 4, core: 2. Of those that a mesh axis runs over, the one named last changes fastest.
Arguments:
- gradient: bfloat16 [4, 2560, 8192], P('dp', None, 'tensor'), may hold values from -6 to 6
- feedback: float32 [4, 2560, 8192], P('dp', None, 'tensor'), may hold values from -4 to 4
- q_start: float32 [8192, 32], P('tensor'), may hold values from -6 to 6
Outputs:
- p_factor: float32 [2560, 32], P('tensor')
- q_factor: float32 [8192, 32], P('tensor')
- decoded: float32 [2560, 8192], P(None, 'tensor')
- residual: float32 [4, 2560, 8192], P('dp', None, 'tensor')
All inputs are finite; a program needn't handle non-finite values.
Results may differ from a plain program's by a relative error of at most 0.0003.
Values sent between devices are 32-bit elements; how exact they have to be, the bound alone decides.
A program may use at most 64 MiB of HBM per device.

v0:
```python
import jax
import jax.numpy as jnp
from jax import lax
from jax.sharding import PartitionSpec as P


def orthonormal(p_sum, gram_matrix):
    factor_low = jnp.linalg.cholesky(gram_matrix)
    return jax.scipy.linalg.solve_triangular(factor_low, p_sum.T, lower=True).T


def local(gradient, feedback, q_start):
    high = lax.Precision.HIGHEST
    merged = gradient[0].astype(jnp.float32) + feedback[0]
    row_block = lax.psum_scatter(
        jnp.dot(merged, q_start, precision=high), "tensor", scatter_dimension=0, tiled=True
    )
    row_block = lax.psum(row_block, "dp")
    gram_matrix = lax.psum(jnp.dot(row_block.T, row_block, precision=high), "tensor")
    p_factor = orthonormal(row_block, gram_matrix)
    basis_all = lax.all_gather(p_factor, "tensor", axis=0, tiled=True)
    q_local = lax.dot_general(merged, basis_all, (((0,), (0,)), ((), ())), precision=high)
    q_factor = lax.psum(q_local, "dp") / lax.axis_size("dp")
    decoded = jnp.dot(basis_all, q_factor.T, precision=high)
    residual = merged - decoded
    return (p_factor, q_factor, decoded, residual[None])


def solution(mesh):
    in_specs = (P("dp", None, "tensor"), P("dp", None, "tensor"), P("tensor", None))
    out_specs = (P("tensor", None), P("tensor", None), P(None, "tensor"), P("dp", None, "tensor"))
    return jax.shard_map(local, mesh=mesh, in_specs=in_specs, out_specs=out_specs, check_vma=False)
```

profile of v0, /device:TPU:0, one launch (start us, length us, event | category | flops | bytes accessed | tf_op | source)
XLA Modules:
  0.0 192.3 jit_solution(12324662725646355803)
XLA Ops:
  7.2 0.0 copy-start
  7.2 0.0 reduce-scatter.4.cloned.1.call-start
  7.2 0.8 copy-done
  8.1 12.6 %fusion.2 = f32[2560,32]{1,0:T(8,128)} fusion(f32[1024,32]{0,1:T(8,128)S(1)} %copy-done, f32[1,2560,1024]{2,1,0:T(8,128)} %param.4, bf16[1,2560,1024]{2,1,0:T(8,128)(2,1)} %param.3), kind=kOutput, calls=%fused_computation.3 | convolution fusion | flops 1011875840 | bytes 16187392
  20.7 0.0 reduce-scatter.4.cloned.1.call-update
  20.7 0.0 all-reduce.2.cloned.1.call-start
  20.8 40.0 %reduce-scatter.4.cloned.1.call-done = f32[320,32]{1,0:T(8,128)} async-done(((f32[2560,32]{1,0:T(8,128)}), f32[320,32]{1,0:T(8,128)}) %reduce-scatter.4.cloned.1.call-update) | async-done | bytes 40976
  60.8 1.0 copy.17
  61.8 19.5 %psum.21 = f32[320,32]{0,1:T(8,128)S(1)} all-reduce(f32[320,32]{0,1:T(8,128)S(1)} %copy.17), channel_id=1, replica_groups=mesh['dp'=4,'tensor'=8] {'dp'}, use_global_device_ids=true, to_apply=%region_1.0 | all-reduce | flops 10240 | bytes 81920 | tf_op jit(solution)/shard_map/psum | solution.py:18
  81.3 0.2 fusion.9
  81.5 22.3 %psum.22 = f32[32,32]{0,1:T(8,128)S(1)} all-reduce(f32[32,32]{0,1:T(8,128)S(1)} %fusion.9), channel_id=1, replica_groups=mesh['dp'=4,'tensor'=8] {'tensor'}, use_global_device_ids=true, to_apply=%region_2.0 | all-reduce | flops 1024 | bytes 8192 | tf_op jit(solution)/shard_map/psum | solution.py:19
  103.8 0.1 copy.13
  103.9 2.9 %cholesky.16 = f32[32,32]{1,0:T(8,128)S(1)} custom-call(f32[32,32]{1,0:T(8,128)S(1)} %fusion.8), custom_call_target="Cholesky" | custom-call | tf_op jit(solution)/shard_map/jit(cholesky)/cholesky | solution.py:8
  106.8 0.6 compare_reduce_fusion
  107.5 0.7 fusion.5
  108.1 2.4 %custom-call.7 = f32[1,32,32]{1,2,0:T(8,128)S(1)} custom-call(f32[1,32,32]{2,1,0:T(8,128)S(1)} %fusion.5), custom_call_target="InvertDiagBlocksLowerTriangular" | custom-call | tf_op jit(solution)/shard_map/jit(_solve_triangular)/triangular_solve | solution.py:9
  110.6 0.3 fusion.6
  110.9 0.0 copy-start.3
  110.9 9.6 %all-gather = f32[8,320,32]{1,2,0:T(8,128)S(1)} all-gather(f32[1,320,32]{1,2,0:T(8,128)S(1)} %bitcast.32), channel_id=1, replica_groups=mesh['dp'=4,'tensor'=8] {'tensor'}, dimensions={0}, use_global_device_ids=true | all-gather | bytes 368640 | tf_op jit(solution)/shard_map/all_gather | solution.py:21
  120.4 0.2 copy.14
  120.7 0.1 reshape.21
  120.8 11.0 %fusion = f32[1024,32]{0,1:T(8,128)} fusion(f32[2560,32]{0,1:T(8,128)S(1)} %reshape.21, f32[1,2560,1024]{2,1,0:T(8,128)} %param.4, bf16[1,2560,1024]{2,1,0:T(8,128)(2,1)} %param.3), kind=kOutput, calls=%fused_computation.1 | convolution fusion | flops 1011875840 | bytes 16187392 | tf_op jit(solution)/shard_map/dot_general | solution.py:22
  131.8 0.0 all-reduce.2.cloned.1.call-update
  131.8 32.1 %all-reduce.2.cloned.1.call-done = f32[1024,32]{0,1:T(8,128)} async-done(((f32[1024,32]{0,1:T(8,128)}), f32[1024,32]{0,1:T(8,128)}) %all-reduce.2.cloned.1.call-update) | async-done | bytes 131088 | tf_op jit(solution)/shard_map/psum | solution.py:23
  163.9 0.9 broadcast_multiply_fusion
  164.8 0.0 copy-start.2
  164.8 0.0 slice-start.1
  164.8 8.5 %fusion.10 = f32[2560,1024]{1,0:T(8,128)S(1)} fusion(f32[2560,32]{0,1:T(8,128)S(1)} %reshape.21, f32[1024,32]{0,1:T(8,128)S(1)} %broadcast_multiply_fusion), kind=kOutput, calls=%fused_computation.19 | convolution fusion | flops 1006632960 | bytes 10944512 | tf_op jit(solution)/shard_map/dot_general | solution.py:24
  173.3 0.0 copy-done.3
  173.4 0.0 copy-start.1
  173.4 12.1 %fusion.4 = f32[1,2560,1024]{2,1,0:T(8,128)} fusion(f32[2560,1024]{1,0:T(8,128)S(1)} %fusion.10, f32[1,2560,1024]{2,1,0:T(8,128)} %param.4, bf16[1,2560,1024]{2,1,0:T(8,128)(2,1)S(1)} %bitcast.31), kind=kLoop, calls=%fused_computation.5 | loop fusion | flops 7864320 | bytes 36700160 | tf_op jit(solution)/shard_map/broadcast_in_dim | solution.py:26
  185.5 0.0 copy-done.1
  (7 shorter events, 0.0 us)
Async XLA Ops:
  7.2 0.9 copy-start
  7.2 53.6 %reduce-scatter.4.cloned.1.call-start = ((), (), s32[]{:S(2)}) async-start(), calls=%async_computation.2 | async-start | bytes 1474560
  20.7 143.1 %all-reduce.2.cloned.1.call-start = ((), (), s32[]{:S(2)}) async-start(), calls=%async_computation.1 | async-start | bytes 262144 | tf_op jit(solution)/shard_map/psum | solution.py:23
  110.9 62.5 %copy-start.3 = (f32[320,32]{0,1:T(8,128)}, f32[320,32]{0,1:T(8,128)S(1)}, u32[]{:S(2)}) copy-start(f32[320,32]{0,1:T(8,128)S(1)} %fusion.6) | copy-start | bytes 122884
  131.8 41.6 %slice-start = ((s8[5242880]{0:T(1024)(128)(4,1)}), s8[1048576]{0:T(1024)(128)(4,1)S(1)}, s32[]{:S(2)}) async-start(s8[5242880]{0:T(1024)(128)(4,1)} %bitcast.30), calls=%async_computation.3 | async-start | bytes 2097152
  164.8 20.7 %copy-start.2 = (f32[1024,32]{0,1:T(8,128)}, f32[1024,32]{0,1:T(8,128)S(1)}, u32[]{:S(2)}) copy-start(f32[1024,32]{0,1:T(8,128)S(1)} %broadcast_multiply_fusion) | copy-start | bytes 393220
  164.8 8.6 %slice-start.1 = ((s8[5242880]{0:T(1024)(128)(4,1)}), s8[4194304]{0:T(1024)(128)(4,1)S(1)}, s32[]{:S(2)}) async-start(s8[5242880]{0:T(1024)(128)(4,1)} %bitcast.30), calls=%async_computation.4 | async-start | bytes 8388608
  173.4 12.1 %copy-start.1 = (f32[2560,1024]{1,0:T(8,128)}, f32[2560,1024]{1,0:T(8,128)S(1)}, u32[]{:S(2)}) copy-start(f32[2560,1024]{1,0:T(8,128)S(1)} %fusion.10) | copy-start | bytes 31457284
Sparse Core Ops, SparseCore 0:
  20.9 39.8 reduce-scatter.3
  131.9 31.8 all-reduce.1
where the time goes:
time: 193 us; the launch traced here: 192 us
  waiting for transfers between devices  72.1 us (37%)
  blocking collectives  51.4 us (27%)
  matrix products  32.6 us (17%)
  other arithmetic  19.7 us (10%)
  between operations  14.2 us (7%)
  local copies, waits for them, and re-layouts  2.32 us (1%)
    unnamed x3, waiting for transfers between devices  40 us
    psum x1, waiting for transfers between devices, local(): q_factor = lax.psum(q_local, 'dp') / lax.axis_size('dp')  32.1 us
    psum x1, blocking collectives, local(): lax.psum(jnp.dot(row_block.T, row_block, precision=high), 'tensor')  22.3 us
    psum x1, blocking collectives, local(): row_block = lax.psum(row_block, 'dp')  19.5 us
    unnamed x1, matrix products  12.6 us
    broadcast_in_dim x1, other arithmetic, local(): return (p_factor, q_factor, decoded, residual[None])  12.1 us
    dot_general x1, matrix products, local(): lax.dot_general(merged, basis_all, (((0,), (0,)), ((), ())), precision=high)  11 us
    all_gather x1, blocking collectives, local(): basis_all = lax.all_gather(p_factor, 'tensor', axis=0, tiled=True)  9.56 us
  transfers between devices with their start and end apart: 2, of which 2 were waited for; matrix products, arithmetic and copies ran while one was open for 0% of the time, Pallas kernels for 0%

commit v1 on v0

v1 whole, which is shorter than its diff:
```python
import functools

import jax
import jax.numpy as jnp
from jax import lax
from jax.experimental import pallas as pl
from jax.experimental.pallas import tpu as pltpu
from jax.sharding import PartitionSpec as P

MESH = pl.DeviceIdType.MESH
HIGH = lax.Precision.HIGHEST
F32 = jnp.float32
BF16 = jnp.bfloat16
NN = (((1,), (0,)), ((), ()))
NT = (((1,), (1,)), ((), ()))


def dot(a, b, dims, precision=None):
    return lax.dot_general(a, b, dims, precision=precision, preferred_element_type=F32)


def halves(x):
    high = x.astype(BF16)
    return high, (x - high.astype(F32)).astype(BF16)


def inverse_factor(gram):
    rank = gram.shape[0]
    row_at = lax.broadcasted_iota(jnp.int32, (rank, rank), 0)
    col_at = lax.broadcasted_iota(jnp.int32, (rank, rank), 1)
    left = gram
    right = jnp.where(row_at == col_at, 1.0, 0.0).astype(F32)
    for j in range(rank):
        pivot = left[j : j + 1, j : j + 1]
        root = lax.rsqrt(pivot)
        root = root * (1.5 - 0.5 * ((pivot * root) * root))
        left_row = left[j : j + 1, :] * root
        right_row = right[j : j + 1, :] * root
        column = left[:, j : j + 1] * root
        left = left - column * left_row
        right = jnp.where(
            row_at == j, right_row, right - jnp.where(row_at > j, column, 0.0) * right_row
        )
    return right


def factors(n_t, n_dp, g_hbm, f_hbm, q_ref, p_out, q_out, g_buf, f_buf, m_high, m_low, part, part_in,
            chunk, chunk_in, p_all, qpart, qpart_in, q_all, load_g, load_f, s1, r1, s2, r2, s3, r3, s4, r4, s5, r5):
    rank, rows = part.shape[1:]
    width = qpart.shape[2]
    t = lax.axis_index("tensor")
    z = lax.axis_index("dp")

    def block(k):
        return pl.ds(pl.multiple_of(lax.rem(t + k, n_t) * rows, rows), rows)

    def loads(k):
        here = block(k)
        return (
            pltpu.make_async_copy(g_hbm.at[here], g_buf.at[here], load_g.at[k]),
            pltpu.make_async_copy(f_hbm.at[here], f_buf.at[here], load_f.at[k]),
        )

    for k in range(1, n_t + 1):
        for copy in loads(k % n_t):
            copy.start()

    barrier = pltpu.get_barrier_semaphore()
    for k in range(1, n_t):
        pl.semaphore_signal(barrier, inc=1, device_id={"tensor": lax.rem(t + k, n_t)}, device_id_type=MESH)
    for k in range(1, n_dp):
        pl.semaphore_signal(barrier, inc=1, device_id={"dp": lax.rem(z + k, n_dp)}, device_id_type=MESH)

    q_high, q_low = halves(q_ref[...].T)
    q_both = jnp.concatenate([q_high, q_low], axis=0)

    pl.semaphore_wait(barrier, n_t - 1 + n_dp - 1)

    def product(k):
        for copy in loads(k):
            copy.wait()
        here = block(k)
        high, low = halves(g_buf[here, :].astype(F32) + f_buf[here, :])
        m_high[here, :] = high
        m_low[here, :] = low
        first = dot(q_both, high, NT)
        return first[:rank] + first[rank:] + dot(q_high, low, NT)

    def send_part(k):
        peer = lax.rem(t + k, n_t)
        return pltpu.make_async_remote_copy(
            part.at[peer], part_in.at[t], s1.at[peer], r1.at[t], device_id={"tensor": peer}, device_id_type=MESH
        )

    for k in range(1, n_t):
        part[lax.rem(t + k, n_t)] = product(k)
        send_part(k).start()
    part_in[t] = product(0)

    def arrived(buf, sem, slot, axis):
        pltpu.make_async_remote_copy(
            buf.at[slot], buf.at[slot], sem.at[slot], sem.at[slot], device_id={axis: slot}, device_id_type=MESH
        ).wait_recv()

    for k in range(1, n_t):
        arrived(part_in, r1, lax.rem(t + k, n_t), "tensor")
    own = part_in[0]
    for k in range(1, n_t):
        own = own + part_in[k]
    chunk[...] = own
    chunk_in[z] = own

    def send_chunk(k):
        peer = lax.rem(z + k, n_dp)
        return pltpu.make_async_remote_copy(
            chunk, chunk_in.at[z], s2.at[peer], r2.at[z], device_id={"dp": peer}, device_id_type=MESH
        )

    for k in range(1, n_dp):
        send_chunk(k).start()
    for k in range(1, n_dp):
        arrived(chunk_in, r2, lax.rem(z + k, n_dp), "dp")
    own = chunk_in[0]
    for k in range(1, n_dp):
        own = own + chunk_in[k]
    p_all[t] = own

    def send_rows(k):
        peer = lax.rem(t + k, n_t)
        return pltpu.make_async_remote_copy(
            p_all.at[t], p_all.at[t], s3.at[peer], r3.at[t], device_id={"tensor": peer}, device_id_type=MESH
        )

    for k in range(1, n_t):
        send_rows(k).start()
    for k in range(1, n_t):
        arrived(p_all, r3, lax.rem(t + k, n_t), "tensor")
    gram = dot(p_all[0], p_all[0], NT, HIGH)
    for k in range(1, n_t):
        gram = gram + dot(p_all[k], p_all[k], NT, HIGH)
    inverse = inverse_factor(gram)
    for k in range(n_t):
        p_out[k] = dot(inverse, p_all[k], NN, HIGH)

    def q_block(c):
        at = pl.ds(pl.multiple_of(c * width, width), width)
        total = jnp.zeros((rank, width), F32)
        for k in range(n_t):
            high, low = halves(p_out[k])
            both = jnp.concatenate([high, low], axis=0)
            first = dot(both, m_high[k * rows : (k + 1) * rows, at], NN)
            total = total + (first[:rank] + first[rank:] + dot(high, m_low[k * rows : (k + 1) * rows, at], NN))
        return total

    def send_qpart(k):
        peer = lax.rem(z + k, n_dp)
        return pltpu.make_async_remote_copy(
            qpart.at[peer], qpart_in.at[z], s4.at[peer], r4.at[z], device_id={"dp": peer}, device_id_type=MESH
        )

    for k in range(1, n_dp):
        peer = lax.rem(z + k, n_dp)
        qpart[peer] = q_block(peer)
        send_qpart(k).start()
    qpart_in[z] = q_block(z)
    for k in range(1, n_dp):
        arrived(qpart_in, r4, lax.rem(z + k, n_dp), "dp")
    total = qpart_in[0]
    for k in range(1, n_dp):
        total = total + qpart_in[k]
    q_all[z] = total * (1.0 / n_dp)

    def send_q(k):
        peer = lax.rem(z + k, n_dp)
        return pltpu.make_async_remote_copy(
            q_all.at[z], q_all.at[z], s5.at[peer], r5.at[z], device_id={"dp": peer}, device_id_type=MESH
        )

    for k in range(1, n_dp):
        send_q(k).start()
    for k in range(1, n_dp):
        arrived(q_all, r5, lax.rem(z + k, n_dp), "dp")
    for c in range(n_dp):
        q_out[c] = q_all[c]

    for k in range(1, n_t):
        send_part(k).wait_send()
        send_rows(k).wait_send()
    for k in range(1, n_dp):
        send_chunk(k).wait_send()
        send_qpart(k).wait_send()
        send_q(k).wait_send()


def decode(n_dp, g_ref, f_ref, p_ref, q_ref, p_out, q_out, d_out, r_out, q_stack):
    step = pl.program_id(0)
    width = q_ref.shape[2]

    @pl.when(step == 0)
    def _():
        for c in range(n_dp):
            at = slice(c * width, (c + 1) * width)
            high, low = halves(q_ref[c])
            q_stack[:, at] = jnp.concatenate([high, high, low], axis=0)
            q_out[at, :] = q_ref[c].T

    @pl.when(step == lax.axis_index("tensor"))
    def _():
        p_out[...] = p_ref[0].T

    high, low = halves(p_ref[0])
    high, low = high.astype(F32), low.astype(F32)
    p_stack = jnp.concatenate([high, low, high], axis=0).T.astype(BF16)
    decoded = dot(p_stack, q_stack[...], NN)
    d_out[...] = decoded
    r_out[...] = (g_ref[...].astype(F32) + f_ref[...]) - decoded


def kernels(n_t, n_dp, gradient, feedback, q_start):
    gradient, feedback = gradient[0], feedback[0]
    total_rows, cols = gradient.shape
    rank = q_start.shape[1]
    rows, width = total_rows // n_t, cols // n_dp
    vmem = pl.BlockSpec(memory_space=pltpu.VMEM)
    hbm = pl.BlockSpec(memory_space=pl.ANY)
    dma = pltpu.SemaphoreType.DMA
    p3, q4 = pl.pallas_call(
        functools.partial(factors, n_t, n_dp),
        out_shape=(
            jax.ShapeDtypeStruct((n_t, rank, rows), F32),
            jax.ShapeDtypeStruct((n_dp, rank, width), F32),
        ),
        in_specs=[hbm, hbm, vmem],
        out_specs=(vmem, vmem),
        scratch_shapes=[
            pltpu.VMEM((total_rows, cols), BF16),
            pltpu.VMEM((total_rows, cols), F32),
            pltpu.VMEM((total_rows, cols), BF16),
            pltpu.VMEM((total_rows, cols), BF16),
            pltpu.VMEM((n_t, rank, rows), F32),
            pltpu.VMEM((n_t, rank, rows), F32),
            pltpu.VMEM((rank, rows), F32),
            pltpu.VMEM((n_dp, rank, rows), F32),
            pltpu.VMEM((n_t, rank, rows), F32),
            pltpu.VMEM((n_dp, rank, width), F32),
            pltpu.VMEM((n_dp, rank, width), F32),
            pltpu.VMEM((n_dp, rank, width), F32),
            dma((n_t,)), dma((n_t,)),
            dma((n_t,)), dma((n_t,)),
            dma((n_dp,)), dma((n_dp,)),
            dma((n_t,)), dma((n_t,)),
            dma((n_dp,)), dma((n_dp,)),
            dma((n_dp,)), dma((n_dp,)),
        ],
        compiler_params=pltpu.CompilerParams(collective_id=0, has_side_effects=True, vmem_limit_bytes=48 << 20),
    )(gradient, feedback, q_start)
    tile = pl.BlockSpec((rows, cols), lambda i: (i, 0))
    p_factor, q_factor, decoded, residual = pl.pallas_call(
        functools.partial(decode, n_dp),
        grid=(n_t,),
        out_shape=(
            jax.ShapeDtypeStruct((rows, rank), F32),
            jax.ShapeDtypeStruct((cols, rank), F32),
            jax.ShapeDtypeStruct((total_rows, cols), F32),
            jax.ShapeDtypeStruct((total_rows, cols), F32),
        ),
        in_specs=[
            tile,
            tile,
            pl.BlockSpec((1, rank, rows), lambda i: (i, 0, 0)),
            pl.BlockSpec((n_dp, rank, width), lambda i: (0, 0, 0)),
        ],
        out_specs=(
            pl.BlockSpec((rows, rank), lambda i: (0, 0)),
            pl.BlockSpec((cols, rank), lambda i: (0, 0)),
            tile,
            tile,
        ),
        scratch_shapes=[pltpu.VMEM((3 * rank, cols), BF16)],
    )(gradient, feedback, p3, q4)
    return p_factor, q_factor, decoded, residual[None]


def plain(n_t, n_dp, gradient, feedback, q_start):
    merged = gradient[0].astype(F32) + feedback[0]
    row_block = lax.psum_scatter(
        jnp.dot(merged, q_start, precision=HIGH), "tensor", scatter_dimension=0, tiled=True
    )
    row_block = lax.psum(row_block, "dp")
    gram = lax.psum(jnp.dot(row_block.T, row_block, precision=HIGH), "tensor")
    factor_low = jnp.linalg.cholesky(gram)
    p_factor = jax.scipy.linalg.solve_triangular(factor_low, row_block.T, lower=True).T
    basis_all = lax.all_gather(p_factor, "tensor", axis=0, tiled=True)
    q_local = lax.dot_general(merged, basis_all, (((0,), (0,)), ((), ())), precision=HIGH)
    q_factor = lax.psum(q_local, "dp") / n_dp
    decoded = jnp.dot(basis_all, q_factor.T, precision=HIGH)
    return p_factor, q_factor, decoded, (merged - decoded)[None]


def local(n_t, n_dp, gradient, feedback, q_start):
    total_rows, cols = gradient.shape[1:]
    fits = total_rows % (16 * n_t) == 0 and cols % (128 * n_dp) == 0 and q_start.shape[1] % 16 == 0
    small = total_rows * cols * 10 <= 36 << 20
    return (kernels if fits and small else plain)(n_t, n_dp, gradient, feedback, q_start)


def solution(mesh):
    n_t, n_dp = mesh.shape["tensor"], mesh.shape["dp"]
    in_specs = (P("dp", None, "tensor"), P("dp", None, "tensor"), P("tensor", None))
    out_specs = (P("tensor", None), P("tensor", None), P(None, "tensor"), P("dp", None, "tensor"))
    step = functools.partial(local, n_t, n_dp)
    return jax.shard_map(step, mesh=mesh, in_specs=in_specs, out_specs=out_specs, check_vma=False)
```

time: 193 us -> 63.6 us (0.33)
  waiting for transfers between devices: 72.1 us -> 0 us
  Pallas kernels: 0 us -> 56.6 us
  blocking collectives: 51.4 us -> 0 us
  matrix products: 32.6 us -> 0 us
  other arithmetic: 19.7 us -> 0 us
  between operations: 14.2 us -> 0.66 us
  local copies, waits for them, and re-layouts: 2.32 us -> 6.01 us
    pallas_call x0 -> x2, Pallas kernels: none -> 56.6 us  [the longest x1 41 us: kernels(): pl.pallas_call(functools.partial(factors, n_t, n_dp), out_shape=(jax.Shap...]
    psum x2 -> x0, blocking collectives: 41.8 us -> none  [the longest x1 22.3 us: local(): lax.psum(jnp.dot(row_block.T, row_block, precision=high), 'tensor')]
    unnamed x3 -> x0, waiting for transfers between devices: 40 us -> none
    psum x1 -> x0, waiting for transfers between devices: 32.1 us -> none  [local(): q_factor = lax.psum(q_local, 'dp') / lax.axis_size('dp')]
    dot_general x3 -> x0, matrix products: 19.7 us -> none  [the longest x1 11 us: local(): lax.dot_general(merged, basis_all, (((0,), (0,)), ((), ())), precision=high)]
    unnamed x1 -> x0, matrix products: 12.6 us -> none
    broadcast_in_dim x1 -> x0, other arithmetic: 12.1 us -> none  [local(): return (p_factor, q_factor, decoded, residual[None])]
    all_gather x1 -> x0, blocking collectives: 9.56 us -> none  [local(): basis_all = lax.all_gather(p_factor, 'tensor', axis=0, tiled=True)]
  transfers between devices with their start and end apart: 2 -> 0, of which waited for: 2 -> 0; matrix products, arithmetic and copies ran while one was open for 0% -> 0% of each run, Pallas kernels for 0% -> 0%
where the time goes in v1:
time: 63.6 us; the launch traced here: 63.3 us
  Pallas kernels  56.6 us (89%)
  local copies, waits for them, and re-layouts  6.01 us (9%)
  between operations  0.66 us (1%)
    pallas_call x1, Pallas kernels, kernels(): pl.pallas_call(functools.partial(factors, n_t, n_dp), out_shape=(jax.Shap...  41 us
    pallas_call x1, Pallas kernels, kernels(): pl.pallas_call(functools.partial(decode, n_dp), grid=(n_t,), out_shape=(j...  15.6 us
    unnamed x7, local copies, waits for them, and re-layouts  6.01 us

profile of v1, /device:TPU:0, one launch (start us, length us, event | category | flops | bytes accessed | tf_op | source)
XLA Modules:
  0.0 63.3 jit_solution(17713617250512259916)
XLA Ops:
  0.6 1.1 %copy.7.q_ref = f32[1024,32]{1,0:T(8,128)S(1)} copy(f32[1024,32]{0,1:T(8,128)} %param.5) | data formatting | bytes 262144 | tf_op args[2]
  1.7 41.0 %shard_map.66 = (f32[8,32,320]{2,1,0:T(8,128)S(1)}, f32[4,32,256]{2,1,0:T(8,128)S(1)}) custom-call(bf16[2560,1024]{1,0:T(8,128)(2,1)} %bitcast.5, f32[2560,1024]{1,0:T(8,128)} %bitcast.3, f32[1024,32]{1,0:T(8,128)S(1)} %copy.7.q_ref), custom_call_target="tpu_custom_call" | custom-call | tf_op jit(solution)/shard_map/pallas_call | solution.py:227
  42.7 0.0 copy-start
  42.8 0.7 %copy-done = f32[8,32,320]{2,1,0:T(8,128)} copy-done((f32[8,32,320]{2,1,0:T(8,128)}, f32[8,32,320]{2,1,0:T(8,128)S(1)}, u32[]{:S(2)}) %copy-start) | copy-done | bytes 327704
  43.5 0.0 copy-start.1
  43.5 0.7 %copy-done.1 = f32[4,32,256]{2,1,0:T(8,128)} copy-done((f32[4,32,256]{2,1,0:T(8,128)}, f32[4,32,256]{2,1,0:T(8,128)S(1)}, u32[]{:S(2)}) %copy-start.1) | copy-done | bytes 131096
  44.1 15.6 %shard_map.67 = (f32[320,32]{1,0:T(8,128)}, f32[1024,32]{1,0:T(8,128)}, f32[2560,1024]{1,0:T(8,128)}, f32[2560,1024]{1,0:T(8,128)}) custom-call(bf16[2560,1024]{1,0:T(8,128)(2,1)} %bitcast.6, f32[2560,1024]{1,0:T(8,128)} %bitcast.4, f32[8,32,320]{2,1,0:T(8,128)} %copy-done, f32[4,32,256]{2,1,0:T(8,128)} %copy-done.1), custom_call_target="tpu_custom_call" | custom-call | tf_op jit(solution)/shard_map/pallas_call | solution.py:258
  59.7 1.6 %copy.8 = f32[320,32]{0,1:T(8,128)} copy(f32[320,32]{1,0:T(8,128)} %get-tuple-element.16) | data formatting | bytes 81920
  61.4 1.9 %copy.9 = f32[1024,32]{0,1:T(8,128)} copy(f32[1024,32]{1,0:T(8,128)} %get-tuple-element.17) | data formatting | bytes 262144
Async XLA Ops:
  42.7 0.7 %copy-start = (f32[8,32,320]{2,1,0:T(8,128)}, f32[8,32,320]{2,1,0:T(8,128)S(1)}, u32[]{:S(2)}) copy-start(f32[8,32,320]{2,1,0:T(8,128)S(1)} %get-tuple-element.10.p_ref) | copy-start | bytes 983044
  43.5 0.7 %copy-start.1 = (f32[4,32,256]{2,1,0:T(8,128)}, f32[4,32,256]{2,1,0:T(8,128)S(1)}, u32[]{:S(2)}) copy-start(f32[4,32,256]{2,1,0:T(8,128)S(1)} %get-tuple-element.11.q_ref) | copy-start | bytes 393220

commit v2 on v1

--- a/solution.py
+++ b/solution.py
@@ -44,8 +44,8 @@
     return right
 
 
-def factors(n_t, n_dp, g_hbm, f_hbm, q_ref, p_out, q_out, g_buf, f_buf, m_high, m_low, part, part_in,
-            chunk, chunk_in, p_all, qpart, qpart_in, q_all, load_g, load_f, s1, r1, s2, r2, s3, r3, s4, r4, s5, r5):
+def factors(n_t, n_dp, g_ref, f_hbm, q_ref, p_own, p_out, q_out, m_out, m_high, m_low, part, part_in,
+            chunk, chunk_in, p_all, p_sum, qpart, qpart_in, q_all, load_f, s1, r1, s2, r2, s3, r3, s4, r4, s5, r5):
     rank, rows = part.shape[1:]
     width = qpart.shape[2]
     t = lax.axis_index("tensor")
@@ -54,16 +54,12 @@
     def block(k):
         return pl.ds(pl.multiple_of(lax.rem(t + k, n_t) * rows, rows), rows)
 
-    def loads(k):
+    def load(k):
         here = block(k)
-        return (
-            pltpu.make_async_copy(g_hbm.at[here], g_buf.at[here], load_g.at[k]),
-            pltpu.make_async_copy(f_hbm.at[here], f_buf.at[here], load_f.at[k]),
-        )
+        return pltpu.make_async_copy(f_hbm.at[here], m_out.at[here], load_f.at[k])
 
     for k in range(1, n_t + 1):
-        for copy in loads(k % n_t):
-            copy.start()
+        load(k % n_t).start()
 
     barrier = pltpu.get_barrier_semaphore()
     for k in range(1, n_t):
@@ -71,16 +67,17 @@
     for k in range(1, n_dp):
         pl.semaphore_signal(barrier, inc=1, device_id={"dp": lax.rem(z + k, n_dp)}, device_id_type=MESH)
 
-    q_high, q_low = halves(q_ref[...].T)
+    q_high, q_low = halves(q_ref[...])
     q_both = jnp.concatenate([q_high, q_low], axis=0)
 
     pl.semaphore_wait(barrier, n_t - 1 + n_dp - 1)
 
     def product(k):
-        for copy in loads(k):
-            copy.wait()
+        load(k).wait()
         here = block(k)
-        high, low = halves(g_buf[here, :].astype(F32) + f_buf[here, :])
+        merged = g_ref[here, :].astype(F32) + m_out[here, :]
+        m_out[here, :] = merged
+        high, low = halves(merged)
         m_high[here, :] = high
         m_low[here, :] = low
         first = dot(q_both, high, NT)
@@ -135,22 +132,19 @@
         send_rows(k).start()
     for k in range(1, n_t):
         arrived(p_all, r3, lax.rem(t + k, n_t), "tensor")
-    gram = dot(p_all[0], p_all[0], NT, HIGH)
-    for k in range(1, n_t):
-        gram = gram + dot(p_all[k], p_all[k], NT, HIGH)
-    inverse = inverse_factor(gram)
     for k in range(n_t):
-        p_out[k] = dot(inverse, p_all[k], NN, HIGH)
+        p_sum[:, k * rows : (k + 1) * rows] = p_all[k]
+    inverse = inverse_factor(dot(p_sum[...], p_sum[...], NT, HIGH))
+    p_own[...] = dot(inverse, p_all[t], NN, HIGH)
+    factor = dot(inverse, p_sum[...], NN, HIGH)
+    p_out[...] = factor
+    p_high, p_low = halves(factor)
+    p_both = jnp.concatenate([p_high, p_low], axis=0)
 
     def q_block(c):
         at = pl.ds(pl.multiple_of(c * width, width), width)
-        total = jnp.zeros((rank, width), F32)
-        for k in range(n_t):
-            high, low = halves(p_out[k])
-            both = jnp.concatenate([high, low], axis=0)
-            first = dot(both, m_high[k * rows : (k + 1) * rows, at], NN)
-            total = total + (first[:rank] + first[rank:] + dot(high, m_low[k * rows : (k + 1) * rows, at], NN))
-        return total
+        first = dot(p_both, m_high[:, at], NN)
+        return first[:rank] + first[rank:] + dot(p_high, m_low[:, at], NN)
 
     def send_qpart(k):
         peer = lax.rem(z + k, n_dp)
@@ -181,7 +175,7 @@
     for k in range(1, n_dp):
         arrived(q_all, r5, lax.rem(z + k, n_dp), "dp")
     for c in range(n_dp):
-        q_out[c] = q_all[c]
+        q_out[:, c * width : (c + 1) * width] = q_all[c]
 
     for k in range(1, n_t):
         send_part(k).wait_send()
@@ -192,28 +186,24 @@
         send_q(k).wait_send()
 
 
-def decode(n_dp, g_ref, f_ref, p_ref, q_ref, p_out, q_out, d_out, r_out, q_stack):
+def decode(m_ref, own_ref, p_ref, q_ref, p_out, q_out, d_out, r_out, q_stack):
     step = pl.program_id(0)
-    width = q_ref.shape[2]
+    rows = d_out.shape[0]
+    here = pl.ds(pl.multiple_of(step * rows, rows), rows)
 
     @pl.when(step == 0)
     def _():
-        for c in range(n_dp):
-            at = slice(c * width, (c + 1) * width)
-            high, low = halves(q_ref[c])
-            q_stack[:, at] = jnp.concatenate([high, high, low], axis=0)
-            q_out[at, :] = q_ref[c].T
-
-    @pl.when(step == lax.axis_index("tensor"))
-    def _():
-        p_out[...] = p_ref[0].T
-
-    high, low = halves(p_ref[0])
+        high, low = halves(q_ref[...])
+        q_stack[...] = jnp.concatenate([high, high, low], axis=0)
+        q_out[...] = q_ref[...]
+        p_out[...] = own_ref[...]
+
+    high, low = halves(p_ref[:, here])
     high, low = high.astype(F32), low.astype(F32)
     p_stack = jnp.concatenate([high, low, high], axis=0).T.astype(BF16)
     decoded = dot(p_stack, q_stack[...], NN)
     d_out[...] = decoded
-    r_out[...] = (g_ref[...].astype(F32) + f_ref[...]) - decoded
+    r_out[...] = m_ref[here, :] - decoded
 
 
 def kernels(n_t, n_dp, gradient, feedback, q_start):
@@ -222,19 +212,19 @@
     rank = q_start.shape[1]
     rows, width = total_rows // n_t, cols // n_dp
     vmem = pl.BlockSpec(memory_space=pltpu.VMEM)
-    hbm = pl.BlockSpec(memory_space=pl.ANY)
+    hbm = pl.BlockSpec(memory_space=pltpu.HBM)
     dma = pltpu.SemaphoreType.DMA
-    p3, q4 = pl.pallas_call(
+    own, basis, right, merged = pl.pallas_call(
         functools.partial(factors, n_t, n_dp),
         out_shape=(
-            jax.ShapeDtypeStruct((n_t, rank, rows), F32),
-            jax.ShapeDtypeStruct((n_dp, rank, width), F32),
+            jax.ShapeDtypeStruct((rank, rows), F32),
+            jax.ShapeDtypeStruct((rank, total_rows), F32),
+            jax.ShapeDtypeStruct((rank, cols), F32),
+            jax.ShapeDtypeStruct((total_rows, cols), F32),
         ),
-        in_specs=[hbm, hbm, vmem],
-        out_specs=(vmem, vmem),
+        in_specs=[vmem, hbm, vmem],
+        out_specs=(vmem, vmem, vmem, vmem),
         scratch_shapes=[
-            pltpu.VMEM((total_rows, cols), BF16),
-            pltpu.VMEM((total_rows, cols), F32),
             pltpu.VMEM((total_rows, cols), BF16),
             pltpu.VMEM((total_rows, cols), BF16),
             pltpu.VMEM((n_t, rank, rows), F32),
@@ -242,43 +232,40 @@
             pltpu.VMEM((rank, rows), F32),
             pltpu.VMEM((n_dp, rank, rows), F32),
             pltpu.VMEM((n_t, rank, rows), F32),
+            pltpu.VMEM((rank, total_rows), F32),
             pltpu.VMEM((n_dp, rank, width), F32),
             pltpu.VMEM((n_dp, rank, width), F32),
             pltpu.VMEM((n_dp, rank, width), F32),
-            dma((n_t,)), dma((n_t,)),
+            dma((n_t,)),
             dma((n_t,)), dma((n_t,)),
             dma((n_dp,)), dma((n_dp,)),
             dma((n_t,)), dma((n_t,)),
             dma((n_dp,)), dma((n_dp,)),
             dma((n_dp,)), dma((n_dp,)),
         ],
-        compiler_params=pltpu.CompilerParams(collective_id=0, has_side_effects=True, vmem_limit_bytes=48 << 20),
-    )(gradient, feedback, q_start)
-    tile = pl.BlockSpec((rows, cols), lambda i: (i, 0))
+        compiler_params=pltpu.CompilerParams(collective_id=0, has_side_effects=True, vmem_limit_bytes=30 << 20),
+    )(gradient, feedback, q_start.T)
+    tile = pl.BlockSpec((256, cols), lambda i: (i, 0))
     p_factor, q_factor, decoded, residual = pl.pallas_call(
-        functools.partial(decode, n_dp),
-        grid=(n_t,),
+        decode,
+        grid=(total_rows // 256,),
         out_shape=(
-            jax.ShapeDtypeStruct((rows, rank), F32),
-            jax.ShapeDtypeStruct((cols, rank), F32),
+            jax.ShapeDtypeStruct((rank, rows), F32),
+            jax.ShapeDtypeStruct((rank, cols), F32),
             jax.ShapeDtypeStruct((total_rows, cols), F32),
             jax.ShapeDtypeStruct((total_rows, cols), F32),
         ),
-        in_specs=[
-            tile,
-            tile,
-            pl.BlockSpec((1, rank, rows), lambda i: (i, 0, 0)),
-            pl.BlockSpec((n_dp, rank, width), lambda i: (0, 0, 0)),
-        ],
+        in_specs=[vmem, vmem, vmem, vmem],
         out_specs=(
-            pl.BlockSpec((rows, rank), lambda i: (0, 0)),
-            pl.BlockSpec((cols, rank), lambda i: (0, 0)),
+            pl.BlockSpec((rank, rows), lambda i: (0, 0)),
+            pl.BlockSpec((rank, cols), lambda i: (0, 0)),
             tile,
             tile,
         ),
         scratch_shapes=[pltpu.VMEM((3 * rank, cols), BF16)],
-    )(gradient, feedback, p3, q4)
-    return p_factor, q_factor, decoded, residual[None]
+        compiler_params=pltpu.CompilerParams(vmem_limit_bytes=24 << 20),
+    )(merged, own, basis, right)
+    return p_factor.T, q_factor.T, decoded, residual[None]
 
 
 def plain(n_t, n_dp, gradient, feedback, q_start):
@@ -299,7 +286,7 @@
 
 def local(n_t, n_dp, gradient, feedback, q_start):
     total_rows, cols = gradient.shape[1:]
-    fits = total_rows % (16 * n_t) == 0 and cols % (128 * n_dp) == 0 and q_start.shape[1] % 16 == 0
+    fits = total_rows % (16 * n_t) == 0 and total_rows % 256 == 0 and cols % (128 * n_dp) == 0 and q_start.shape[1] % 16 == 0
     small = total_rows * cols * 10 <= 36 << 20
     return (kernels if fits and small else plain)(n_t, n_dp, gradient, feedback, q_start)
 

time: 63.6 us -> 53.7 us (0.84)
  Pallas kernels: 56.6 us -> 49.5 us
  local copies, waits for them, and re-layouts: 6.01 us -> 3.38 us
    pallas_call x1, Pallas kernels: 15.6 us -> 8.9 us  [kernels(): pl.pallas_call(decode, grid=(total_rows // 256,), out_shape=(jax.ShapeDty...]
    unnamed x7 -> x4, local copies, waits for them, and re-layouts: 6.01 us -> 3.38 us
where the time goes in v2:
time: 53.7 us; the launch traced here: 53.5 us
  Pallas kernels  49.5 us (92%)
  local copies, waits for them, and re-layouts  3.38 us (6%)
  between operations  0.65 us (1%)
    pallas_call x1, Pallas kernels, kernels(): pl.pallas_call(functools.partial(factors, n_t, n_dp), out_shape=(jax.Shap...  40.6 us
    pallas_call x1, Pallas kernels, kernels(): pl.pallas_call(decode, grid=(total_rows // 256,), out_shape=(jax.ShapeDty...  8.9 us
    unnamed x4, local copies, waits for them, and re-layouts  3.38 us

profile of v2, /device:TPU:0, one launch (start us, length us, event | category | flops | bytes accessed | tf_op | source)
XLA Modules:
  0.0 53.5 jit_solution(9418607122735734385)
XLA Ops:
  0.6 0.0 copy-start
  0.6 2.5 %copy-done = bf16[1,2560,1024]{2,1,0:T(8,128)(2,1)S(1)} copy-done((bf16[1,2560,1024]{2,1,0:T(8,128)(2,1)S(1)}, bf16[1,2560,1024]{2,1,0:T(8,128)(2,1)}, u32[]{:S(2)}) %copy-start) | copy-done | bytes 5242904
  3.1 0.0 copy-start.1
  3.1 0.9 %copy-done.1 = f32[1024,32]{0,1:T(8,128)S(1)} copy-done((f32[1024,32]{0,1:T(8,128)S(1)}, f32[1024,32]{0,1:T(8,128)}, u32[]{:S(2)}) %copy-start.1) | copy-done | bytes 131096
  4.0 40.6 %shard_map.66 = (f32[32,320]{1,0:T(8,128)S(1)}, f32[32,2560]{1,0:T(8,128)S(1)}, f32[32,1024]{1,0:T(8,128)S(1)}, f32[2560,1024]{1,0:T(8,128)S(1)}) custom-call(bf16[2560,1024]{1,0:T(8,128)(2,1)S(1)} %bitcast.6, f32[2560,1024]{1,0:T(8,128)} %bitcast.8, f32[32,1024]{1,0:T(8,128)S(1)} %bitcast.7), custom_call_target="tpu_custom_call" | custom-call | tf_op jit(solution)/shard_map/pallas_call | solution.py:217
  44.6 8.9 %shard_map.67 = (f32[32,320]{1,0:T(8,128)}, f32[32,1024]{1,0:T(8,128)}, f32[2560,1024]{1,0:T(8,128)}, f32[2560,1024]{1,0:T(8,128)}) custom-call(f32[2560,1024]{1,0:T(8,128)S(1)} %get-tuple-element.12.m_ref, f32[32,320]{1,0:T(8,128)S(1)} %get-tuple-element.13.own_ref, f32[32,2560]{1,0:T(8,128)S(1)} %get-tuple-element.14.p_ref, ...), custom_call_target="tpu_custom_call" | custom-call | tf_op jit(solution)/shard_map/pallas_call | solution.py:249
Async XLA Ops:
  0.6 2.5 %copy-start = (bf16[1,2560,1024]{2,1,0:T(8,128)(2,1)S(1)}, bf16[1,2560,1024]{2,1,0:T(8,128)(2,1)}, u32[]{:S(2)}) copy-start(bf16[1,2560,1024]{2,1,0:T(8,128)(2,1)} %param.3) | copy-start | bytes 15728644
  3.1 0.9 %copy-start.1 = (f32[1024,32]{0,1:T(8,128)S(1)}, f32[1024,32]{0,1:T(8,128)}, u32[]{:S(2)}) copy-start(f32[1024,32]{0,1:T(8,128)} %param.5) | copy-start | bytes 393220
